TPU v7x, 256 devices: a whole 4x4x8 slice. The times are simulated.
256 devices in a mesh: feat: 8 (over y, core), dom: 32 (over x, z).
Axes of the slice: x: 4, y: 4, z: 8, core: 2. Of those that a mesh axis runs over, the one named last changes fastest.
Arguments:
- features: bfloat16 [131072, 128], P('dom'), may hold values from -6 to 6
- w_input: bfloat16 [128, 256], P(None, 'feat'), may hold values from -0.5 to 0.5
- layer_weights: bfloat16 [4, 256, 256], replicated, may hold values from -0.375 to 0.375
- history: bfloat16 [4, 131072, 256], P(None, 'dom', 'feat'), may hold values from 0 to 2
- tile_values: bfloat16 [1024, 6, 128, 128], P('dom'), may hold values from -0.21875 to 0.21875
- tile_columns: int32 [1024, 6], P('dom'), may hold values from 0 to 159, as said below
- send_rows: int32 [32, 32, 512], P('dom'), may hold values from 0 to 4095
- send_counts: int32 [32, 32], P('dom'), may hold values from 0 to 512, as said below
Outputs:
- pushed: bfloat16 [4, 131072, 256], P(None, 'dom', 'feat')
- final_rows: bfloat16 [131072, 256], P('dom', 'feat')
Inputs may be any that keep to these rules, and one draw needn't show every extreme that they name: `tile_columns`: per row of tiles the first 2 entries lie below 4096 / 128 (own rows), the others at or above it (halo slots); every halo column tile of every partition is named somewhere. `send_counts`: A partition sends nothing to itself; in every draw some destination receives exactly 512 rows from every other partition.
All inputs are finite; a program needn't handle non-finite values.
Results may differ from a plain program's by a relative error of at most 0.0052.
Values may be sent and summed in bfloat16 or wider, within the bound.
A program may use at most 128 MiB of HBM per device.

v0:
```python
import math

import jax
import jax.numpy as jnp
from jax import lax
from jax.sharding import PartitionSpec as P

LAYERS = 4


ALPHA = 0.1
LAMBDA_DECAY = 0.5


def propagate(own_rows, halo_rows, values, columns, tile_size):
    slice_width = own_rows.shape[1]
    combined = jnp.concatenate([own_rows, halo_rows], axis=0)
    tile_count = combined.shape[0] // tile_size
    flat_tiles = combined.reshape(tile_count, tile_size * slice_width)
    row_tiles, per_row = columns.shape
    selector = (
        columns.reshape(row_tiles * per_row, 1) == jnp.arange(tile_count, dtype=jnp.int32)[None, :]
    ).astype(jnp.bfloat16)
    picked = jnp.dot(selector, flat_tiles, preferred_element_type=jnp.float32).astype(jnp.bfloat16)
    picked = picked.reshape(row_tiles, per_row, tile_size, slice_width)
    summed = jnp.einsum("rkab,rkbf->raf", values, picked, preferred_element_type=jnp.float32)
    return summed.reshape(own_rows.shape[0], slice_width)


def on_device(
    features, w_input, layer_weights, history, tile_values, tile_columns, send_rows, send_counts
):
    initial = jnp.maximum(
        jnp.dot(features, w_input, preferred_element_type=jnp.float32), 0.0
    ).astype(jnp.bfloat16)
    nodes_local, slice_width = initial.shape
    peer_count = send_rows.shape[1]
    slot_count = send_rows.shape[2]
    tile_size = tile_values.shape[-1]
    feat_count = lax.axis_size("feat")
    targets = send_rows[0]
    live_slots = (jnp.arange(slot_count)[None, :] < send_counts[0][:, None])[:, :, None]
    zero_value = jnp.zeros((), jnp.bfloat16)
    packed = jnp.where(live_slots[None], history[:, targets], zero_value)
    arrived = lax.all_to_all(packed, "dom", split_axis=1, concat_axis=1, tiled=True)
    halo_list = [
        arrived[level].reshape(peer_count * slot_count, slice_width) for level in range(LAYERS)
    ]
    pushed = []
    current = initial
    for layer_index in range(LAYERS):
        beta_layer = math.log(LAMBDA_DECAY / (layer_index + 1) + 1.0)
        weight = layer_weights[layer_index]
        aggregated = propagate(
            current, halo_list[layer_index], tile_values, tile_columns, tile_size
        )
        blended = ((1.0 - ALPHA) * aggregated + ALPHA * initial.astype(jnp.float32)).astype(
            jnp.bfloat16
        )
        blended = lax.optimization_barrier(blended)
        pushed.append(current)
        stacked = blended.reshape(feat_count, nodes_local // feat_count, slice_width)
        node_block = lax.all_to_all(stacked, "feat", split_axis=0, concat_axis=2, tiled=True)[0]
        product = jnp.dot(node_block, weight, preferred_element_type=jnp.float32)
        fresh = jnp.maximum(
            (1.0 - beta_layer) * node_block.astype(jnp.float32) + beta_layer * product, 0.0
        )
        result = lax.all_to_all(
            fresh.astype(jnp.bfloat16)[None], "feat", split_axis=2, concat_axis=0, tiled=True
        )
        current = result.reshape(nodes_local, slice_width)
    return (jnp.stack(pushed), current)


def solution(mesh):
    placed = (
        P("dom", None),
        P(None, "feat"),
        P(),
        P(None, "dom", "feat"),
        P("dom", None, None, None),
        P("dom", None),
        P("dom", None, None),
        P("dom", None),
    )
    return jax.shard_map(
        on_device,
        mesh=mesh,
        in_specs=placed,
        out_specs=(P(None, "dom", "feat"), P("dom", "feat")),
        check_vma=False,
    )
```

profile of v0, /device:TPU:1, one launch (start us, length us, event | category | flops | bytes accessed | tf_op | source)
XLA Modules:
  0.0 478.7 jit_solution(14414544784776946450)
XLA Ops:
  0.7 6.2 %copy.87 = bf16[4,4096,32]{2,0,1:T(4,128)(2,1)} copy(bf16[4,4096,32]{1,2,0:T(8,128)(2,1)} %param.11) | data formatting | bytes 2097152 | tf_op args[3]
  7.0 114.8 %gather_fusion = bf16[16384,4,32]{2,1,0:T(4,128)(2,1)} fusion(bf16[4,4096,32]{2,0,1:T(4,128)(2,1)} %copy.87, s32[16384]{0:T(1024)S(1)} %broadcast_clamp_fusion), kind=kCustom, calls=%fused_computation | custom fusion | bytes 8454144 | tf_op jit(solution)/shard_map/gather | solution.py:44
  121.8 20.9 %copy.88 = bf16[32,512,4,32]{1,3,2,0:T(8,128)(2,1)} copy(bf16[32,512,4,32]{3,2,1,0:T(4,128)(2,1)} %bitcast.219) | data formatting | bytes 8388608 | tf_op jit(solution)/shard_map/gather | solution.py:44
  142.7 4.5 select_bitcast_fusion
  147.2 12.1 %all-to-all-start = ((bf16[4,32,512,32]{2,3,0,1:T(8,128)(2,1)}), bf16[4,32,512,32]{2,3,0,1:T(8,128)(2,1)}, u32[]{:S(2)}, u32[]{:S(2)}) async-start(bf16[4,32,512,32]{2,3,0,1:T(8,128)(2,1)} %select_bitcast_fusion), calls=%async_computation | async-start | bytes 8388608 | tf_op jit(solution)/shard_map/all_to_all | solution.py:45
  160.0 91.9 %all-to-all-done = bf16[4,32,512,32]{2,3,0,1:T(8,128)(2,1)} async-done(((bf16[4,32,512,32]{2,3,0,1:T(8,128)(2,1)}), bf16[4,32,512,32]{2,3,0,1:T(8,128)(2,1)}, u32[]{:S(2)}, u32[]{:S(2)}) %all-to-all-start) | async-done | bytes 4194336 | tf_op jit(solution)/shard_map/all_to_all | solution.py:45
  251.9 4.1 fusion.42
  256.2 4.0 copy.90
  260.2 8.0 %reshape.131 = bf16[160,4096]{1,0:T(8,128)(2,1)} reshape(bf16[20480,32]{1,0:T(8,128)(2,1)} %copy.90) | data formatting | bytes 2621440 | tf_op jit(solution)/shard_map/reshape | solution.py:19
  268.3 1.9 convolution_convert_fusion.3
  270.2 6.2 %reshape.132 = bf16[32,6,128,32]{3,2,1,0:T(8,128)(2,1)} reshape(bf16[192,4096]{1,0:T(8,128)(2,1)S(1)} %convolution_convert_fusion.3) | data formatting | bytes 3145728 | tf_op jit(solution)/shard_map/reshape | solution.py:25
  276.4 6.7 %fusion.10 = f32[32,4,8,128]{3,2,1,0:T(8,128)S(1)} fusion(bf16[32,6,128,32]{3,2,1,0:T(8,128)(2,1)} %reshape.132, bf16[32,6,128,128]{3,2,1,0:T(8,128)(2,1)} %param.12), kind=kOutput, calls=%fused_computation.29 | convolution fusion | flops 201457664 | bytes 8388608 | tf_op jit(solution)/shard_map/rkab,rkbf->raf/dot_general | solution.py:26
  283.2 16.3 %all_to_all.125 = bf16[8,512,32]{1,2,0:T(8,128)(2,1)S(1)} all-to-all(bf16[8,512,32]{1,2,0:T(8,128)(2,1)S(1)} %bitcast.255), channel_id=1, replica_groups=mesh['feat'=8,'dom'=32] {'feat'}, dimensions={0} | all-to-all | bytes 524288 | tf_op jit(solution)/shard_map/all_to_all | solution.py:63
  299.6 1.2 fusion.24
  301.8 2.2 reduce
  304.9 4.4 all-to-all-start.2
  309.4 6.4 %all-to-all-done.2 = bf16[8,2,8192]{2,1,0:T(2,128)(2,1)S(1)} async-done(((bf16[8,2,8192]{2,1,0:T(2,128)(2,1)}), bf16[8,2,8192]{2,1,0:T(2,128)(2,1)S(1)}, u32[]{:S(2)}, u32[]{:S(2)}) %all-to-all-start.2) | async-done | bytes 262176 | tf_op jit(solution)/shard_map/all_to_all | solution.py:68
  316.2 4.0 copy.99
  320.2 8.0 %reshape.135 = bf16[160,4096]{1,0:T(8,128)(2,1)} reshape(bf16[20480,32]{1,0:T(8,128)(2,1)} %copy.99) | data formatting | bytes 2621440 | tf_op jit(solution)/shard_map/reshape | solution.py:19
  328.2 1.9 convolution_convert_fusion.2
  330.2 6.2 %reshape.136 = bf16[32,6,128,32]{3,2,1,0:T(8,128)(2,1)} reshape(bf16[192,4096]{1,0:T(8,128)(2,1)S(1)} %convolution_convert_fusion.2) | data formatting | bytes 3145728 | tf_op jit(solution)/shard_map/reshape | solution.py:25
  336.4 6.7 %fusion.12 = f32[32,4,8,128]{3,2,1,0:T(8,128)S(1)} fusion(bf16[32,6,128,32]{3,2,1,0:T(8,128)(2,1)} %reshape.136, bf16[32,6,128,128]{3,2,1,0:T(8,128)(2,1)} %param.12), kind=kOutput, calls=%fused_computation.31 | convolution fusion | flops 201457664 | bytes 8388608 | tf_op jit(solution)/shard_map/rkab,rkbf->raf/dot_general | solution.py:26
  343.2 10.0 %all_to_all.126 = bf16[8,512,32]{1,2,0:T(8,128)(2,1)S(1)} all-to-all(bf16[8,512,32]{1,2,0:T(8,128)(2,1)S(1)} %bitcast.256), channel_id=1, replica_groups=mesh['feat'=8,'dom'=32] {'feat'}, dimensions={0} | all-to-all | bytes 524288 | tf_op jit(solution)/shard_map/all_to_all | solution.py:63
  353.4 1.2 fusion.23
  355.0 2.2 reduce.1
  358.1 4.4 all-to-all-start.4
  362.6 6.4 %all-to-all-done.4 = bf16[8,2,8192]{2,1,0:T(2,128)(2,1)S(1)} async-done(((bf16[8,2,8192]{2,1,0:T(2,128)(2,1)}), bf16[8,2,8192]{2,1,0:T(2,128)(2,1)S(1)}, u32[]{:S(2)}, u32[]{:S(2)}) %all-to-all-start.4) | async-done | bytes 262176 | tf_op jit(solution)/shard_map/all_to_all | solution.py:68
  369.4 4.0 copy.108
  373.4 8.0 %reshape.139 = bf16[160,4096]{1,0:T(8,128)(2,1)} reshape(bf16[20480,32]{1,0:T(8,128)(2,1)} %copy.108) | data formatting | bytes 2621440 | tf_op jit(solution)/shard_map/reshape | solution.py:19
  381.5 1.9 convolution_convert_fusion.1
  383.4 6.2 %reshape.140 = bf16[32,6,128,32]{3,2,1,0:T(8,128)(2,1)} reshape(bf16[192,4096]{1,0:T(8,128)(2,1)S(1)} %convolution_convert_fusion.1) | data formatting | bytes 3145728 | tf_op jit(solution)/shard_map/reshape | solution.py:25
  389.6 6.7 %fusion.14 = f32[32,4,8,128]{3,2,1,0:T(8,128)S(1)} fusion(bf16[32,6,128,32]{3,2,1,0:T(8,128)(2,1)} %reshape.140, bf16[32,6,128,128]{3,2,1,0:T(8,128)(2,1)} %param.12), kind=kOutput, calls=%fused_computation.33 | convolution fusion | flops 201457664 | bytes 8388608 | tf_op jit(solution)/shard_map/rkab,rkbf->raf/dot_general | solution.py:26
  396.4 10.0 %all_to_all.127 = bf16[8,512,32]{1,2,0:T(8,128)(2,1)S(1)} all-to-all(bf16[8,512,32]{1,2,0:T(8,128)(2,1)S(1)} %bitcast.257), channel_id=1, replica_groups=mesh['feat'=8,'dom'=32] {'feat'}, dimensions={0} | all-to-all | bytes 524288 | tf_op jit(solution)/shard_map/all_to_all | solution.py:63
  406.6 1.2 fusion.22
  408.3 2.2 reduce.2
  411.3 4.4 all-to-all-start.6
  415.8 6.4 %all-to-all-done.6 = bf16[8,2,8192]{2,1,0:T(2,128)(2,1)S(1)} async-done(((bf16[8,2,8192]{2,1,0:T(2,128)(2,1)}), bf16[8,2,8192]{2,1,0:T(2,128)(2,1)S(1)}, u32[]{:S(2)}, u32[]{:S(2)}) %all-to-all-start.6) | async-done | bytes 262176 | tf_op jit(solution)/shard_map/all_to_all | solution.py:68
  423.3 4.0 copy.117
  427.3 8.0 %reshape.143 = bf16[160,4096]{1,0:T(8,128)(2,1)} reshape(bf16[20480,32]{1,0:T(8,128)(2,1)} %copy.117) | data formatting | bytes 2621440 | tf_op jit(solution)/shard_map/reshape | solution.py:19
  435.3 1.9 convolution_convert_fusion
  437.3 6.2 %reshape.144 = bf16[32,6,128,32]{3,2,1,0:T(8,128)(2,1)} reshape(bf16[192,4096]{1,0:T(8,128)(2,1)S(1)} %convolution_convert_fusion) | data formatting | bytes 3145728 | tf_op jit(solution)/shard_map/reshape | solution.py:25
  443.5 6.7 %fusion.16 = f32[32,4,8,128]{3,2,1,0:T(8,128)S(1)} fusion(bf16[32,6,128,32]{3,2,1,0:T(8,128)(2,1)} %reshape.144, bf16[32,6,128,128]{3,2,1,0:T(8,128)(2,1)} %param.12), kind=kOutput, calls=%fused_computation.35 | convolution fusion | flops 201457664 | bytes 8388608 | tf_op jit(solution)/shard_map/rkab,rkbf->raf/dot_general | solution.py:26
  451.0 4.4 all-to-all-start.7
  455.4 6.4 %all-to-all-done.7 = bf16[8,512,32]{1,2,0:T(8,128)(2,1)S(1)} async-done(((bf16[8,512,32]{1,2,0:T(8,128)(2,1)}), bf16[8,512,32]{1,2,0:T(8,128)(2,1)S(1)}, u32[]{:S(2)}, u32[]{:S(2)}) %all-to-all-start.7) | async-done | bytes 262176 | tf_op jit(solution)/shard_map/all_to_all | solution.py:63
  462.0 1.2 fusion.21
  463.7 2.3 reduce.3
  466.8 4.4 all-to-all-start.8
  472.3 5.4 %all-to-all-done.8 = bf16[8,2,8192]{2,1,0:T(2,128)(2,1)S(1)} async-done(((bf16[8,2,8192]{2,1,0:T(2,128)(2,1)}), bf16[8,2,8192]{2,1,0:T(2,128)(2,1)S(1)}, u32[]{:S(2)}, u32[]{:S(2)}) %all-to-all-start.8) | async-done | bytes 262176 | tf_op jit(solution)/shard_map/all_to_all | solution.py:68
  (74 shorter events, 12.8 us)
Async XLA Ops:
  0.6 158.9 %copy-start = (bf16[4096,128]{1,0:T(8,128)(2,1)S(1)}, bf16[4096,128]{1,0:T(8,128)(2,1)}, u32[]{:S(2)}) copy-start(bf16[4096,128]{1,0:T(8,128)(2,1)} %param.8) | copy-start | bytes 3145732
  0.6 6.2 %copy-start.7 = (s32[1,32,512]{2,1,0:T(8,128)S(1)}, s32[1,32,512]{2,1,0:T(8,128)}, u32[]{:S(2)}) copy-start(s32[1,32,512]{2,1,0:T(8,128)} %param.14) | copy-start | bytes 196612
  121.8 20.9 %copy-start.10 = (s32[1,32]{1,0:T(1,128)S(1)}, s32[1,32]{1,0:T(1,128)}, u32[]{:S(2)}) copy-start(s32[1,32]{1,0:T(1,128)} %param.15) | copy-start | bytes 388
  147.2 12.1 %copy-start.9 = (s32[32,6]{0,1:T(8,128)S(1)}, s32[32,6]{0,1:T(8,128)}, u32[]{:S(2)}) copy-start(s32[32,6]{0,1:T(8,128)} %param.13) | copy-start | bytes 2308
  147.2 12.3 %copy-start.8 = (bf16[128,32]{0,1:T(8,128)(2,1)S(1)}, bf16[128,32]{0,1:T(8,128)(2,1)}, u32[]{:S(2)}) copy-start(bf16[128,32]{0,1:T(8,128)(2,1)} %param.9) | copy-start | bytes 24580
  147.2 104.7 %all-to-all-start = ((bf16[4,32,512,32]{2,3,0,1:T(8,128)(2,1)}), bf16[4,32,512,32]{2,3,0,1:T(8,128)(2,1)}, u32[]{:S(2)}, u32[]{:S(2)}) async-start(bf16[4,32,512,32]{2,3,0,1:T(8,128)(2,1)} %select_bitcast_fusion), calls=%async_computation | async-start | bytes 8388608 | tf_op jit(solution)/shard_map/all_to_all | solution.py:45
  283.2 26.1 %copy-start.4 = (bf16[1,32,512,32]{2,3,0,1:T(8,128)(2,1)S(1)}, bf16[1,32,512,32]{2,3,0,1:T(8,128)(2,1)}, u32[]{:S(2)}) copy-start(bf16[1,32,512,32]{2,3,0,1:T(8,128)(2,1)} %get-tuple-element.4) | copy-start | bytes 3145732
  304.9 10.9 %all-to-all-start.2 = ((bf16[8,2,8192]{2,1,0:T(2,128)(2,1)}), bf16[8,2,8192]{2,1,0:T(2,128)(2,1)S(1)}, u32[]{:S(2)}, u32[]{:S(2)}) async-start(bf16[8,2,8192]{2,1,0:T(2,128)(2,1)} %reshape.160), calls=%async_computation.2 | async-start | bytes 524288 | tf_op jit(solution)/shard_map/all_to_all | solution.py:68
  343.2 19.3 %copy-start.3 = (bf16[1,32,512,32]{2,3,0,1:T(8,128)(2,1)S(1)}, bf16[1,32,512,32]{2,3,0,1:T(8,128)(2,1)}, u32[]{:S(2)}) copy-start(bf16[1,32,512,32]{2,3,0,1:T(8,128)(2,1)} %get-tuple-element.3) | copy-start | bytes 3145732
  358.1 10.9 %all-to-all-start.4 = ((bf16[8,2,8192]{2,1,0:T(2,128)(2,1)}), bf16[8,2,8192]{2,1,0:T(2,128)(2,1)S(1)}, u32[]{:S(2)}, u32[]{:S(2)}) async-start(bf16[8,2,8192]{2,1,0:T(2,128)(2,1)} %reshape.162), calls=%async_computation.4 | async-start | bytes 524288 | tf_op jit(solution)/shard_map/all_to_all | solution.py:68
  396.4 19.3 %copy-start.2 = (bf16[1,32,512,32]{2,3,0,1:T(8,128)(2,1)S(1)}, bf16[1,32,512,32]{2,3,0,1:T(8,128)(2,1)}, u32[]{:S(2)}) copy-start(bf16[1,32,512,32]{2,3,0,1:T(8,128)(2,1)} %get-tuple-element.2) | copy-start | bytes 3145732
  411.3 10.9 %all-to-all-start.6 = ((bf16[8,2,8192]{2,1,0:T(2,128)(2,1)}), bf16[8,2,8192]{2,1,0:T(2,128)(2,1)S(1)}, u32[]{:S(2)}, u32[]{:S(2)}) async-start(bf16[8,2,8192]{2,1,0:T(2,128)(2,1)} %reshape.164), calls=%async_computation.6 | async-start | bytes 524288 | tf_op jit(solution)/shard_map/all_to_all | solution.py:68
  422.5 0.7 copy-start.5
  450.2 5.2 %copy-start.6 = (bf16[1,512,256]{1,2,0:T(8,128)(2,1)S(1)}, bf16[1,512,256]{1,2,0:T(8,128)(2,1)}, u32[]{:S(2)}) copy-start(bf16[1,512,256]{1,2,0:T(8,128)(2,1)} %copy-done.5) | copy-start | bytes 786436
  451.0 10.9 %all-to-all-start.7 = ((bf16[8,512,32]{1,2,0:T(8,128)(2,1)}), bf16[8,512,32]{1,2,0:T(8,128)(2,1)S(1)}, u32[]{:S(2)}, u32[]{:S(2)}) async-start(bf16[8,512,32]{1,2,0:T(8,128)(2,1)} %bitcast.215), calls=%async_computation.7 | async-start | bytes 524288 | tf_op jit(solution)/shard_map/all_to_all | solution.py:63
  463.6 15.1 %copy-start.1 = (bf16[4096,128]{1,0:T(8,128)(2,1)S(1)}, bf16[4096,128]{1,0:T(8,128)(2,1)}, u32[]{:S(2)}) copy-start(bf16[4096,128]{1,0:T(8,128)(2,1)} %param.8) | copy-start | bytes 3145732
  466.8 10.8 %all-to-all-start.8 = ((bf16[8,2,8192]{2,1,0:T(2,128)(2,1)}), bf16[8,2,8192]{2,1,0:T(2,128)(2,1)S(1)}, u32[]{:S(2)}, u32[]{:S(2)}) async-start(bf16[8,2,8192]{2,1,0:T(2,128)(2,1)} %reshape.166), calls=%async_computation.8 | async-start | bytes 524288 | tf_op jit(solution)/shard_map/all_to_all | solution.py:68
where the time goes:
time: 481 us; the launch traced here: 479 us
  local copies, waits for them, and re-layouts  230 us (48%)
  waiting for transfers between devices  123 us (26%)
  matrix products  39.6 us (8%)
  blocking collectives  36.4 us (8%)
  starting transfers between devices  33.9 us (7%)
  other arithmetic  15.2 us (3%)
    gather x2, local copies, waits for them, and re-layouts, on_device(): packed = jnp.where(live_slots[None], history[:, targets], zero_value)  136 us
    all_to_all x1, waiting for transfers between devices, on_device(): lax.all_to_all(packed, 'dom', split_axis=1, concat_axis=1, tiled=True)  91.9 us
    all_to_all x3, blocking collectives, on_device(): lax.all_to_all(stacked, 'feat', split_axis=0, concat_axis=2, tiled=True)[0]  36.4 us
    reshape x4, local copies, waits for them, and re-layouts, propagate(): flat_tiles = combined.reshape(tile_count, tile_size * slice_width)  32 us
    dot_general x4, matrix products, propagate(): jnp.einsum('rkab,rkbf->raf', values, picked, preferred_element_type=jnp.f...  26.8 us
    reshape x4, local copies, waits for them, and re-layouts, propagate(): picked = picked.reshape(row_tiles, per_row, tile_size, slice_width)  24.9 us
    all_to_all x4, waiting for transfers between devices, on_device(): lax.all_to_all(fresh.astype(jnp.bfloat16)[None], 'feat', split_axis=2, co...  24.6 us
    all_to_all x4, starting transfers between devices, on_device(): lax.all_to_all(fresh.astype(jnp.bfloat16)[None], 'feat', split_axis=2, co...  17.4 us
  transfers between devices with their start and end apart: 6, of which 6 were waited for; matrix products, arithmetic and copies ran while one was open for 0% of the time, Pallas kernels for 0%

commit v1 on v0

v1 whole, which is shorter than its diff:
```python
import functools
import math

import jax
import jax.numpy as jnp
from jax import lax
from jax.experimental import pallas as pl
from jax.experimental.pallas import tpu as pltpu
from jax.sharding import PartitionSpec as P

MESH = pl.DeviceIdType.MESH
LAYERS = 4
ALPHA = 0.1
LAMBDA_DECAY = 0.5
TILE = 128
LANES = 128
PACK = 4
WIDTH = 32
NFEAT = 8
GROUPS = 8
CAP = 512
NODES_DEV = 4096
F = 256
K = 6
BF = jnp.bfloat16
F32 = jnp.float32


def lane_ids(rows):
    return lax.broadcasted_iota(jnp.int32, (rows, LANES), 1)


def swap_blocks(parts):
    x0, x1, x2, x3 = parts
    lane = lane_ids(x0.shape[0])
    low = lane < 64
    even = (lane & 32) == 0
    a0 = jnp.where(low, x0, pltpu.roll(x2, 64, 1))
    a2 = jnp.where(low, pltpu.roll(x0, 64, 1), x2)
    a1 = jnp.where(low, x1, pltpu.roll(x3, 64, 1))
    a3 = jnp.where(low, pltpu.roll(x1, 64, 1), x3)
    y0 = jnp.where(even, a0, pltpu.roll(a1, 32, 1))
    y1 = jnp.where(even, pltpu.roll(a0, 96, 1), a1)
    y2 = jnp.where(even, a2, pltpu.roll(a3, 32, 1))
    y3 = jnp.where(even, pltpu.roll(a2, 96, 1), a3)
    return y0, y1, y2, y3


def fill_table(table_t, table):
    def block(i, carry):
        start = pl.multiple_of(i * TILE, TILE)
        part = table_t[:, pl.ds(start, TILE)].astype(F32)
        table[pl.ds(start, TILE), :] = part.T
        return carry

    lax.fori_loop(0, NODES_DEV // TILE, block, 0)
    table[pl.ds(NODES_DEV, 8), :] = jnp.zeros((8, LANES), F32)


def gather_rows(rows, table, picked, dest):
    for j in range(CAP):
        picked[pl.ds(j, 1), :] = table[pl.ds(rows[dest, j], 1), :]


def pack_rows(picked, packed, dest):
    for c in range(4):
        parts = [picked[pl.ds(t * TILE + c * 32, 32), :] for t in range(PACK)]
        for level, part in enumerate(swap_blocks(parts)):
            packed[level, dest, pl.ds(c * 32, 32), :] = part.astype(BF)


def gather_kernel(n_dom, rows, table_t, packed, table, picked):
    fill_table(table_t, table)

    def one(dest, carry):
        gather_rows(rows, table, picked, dest)
        pack_rows(picked, packed, dest)
        return carry

    lax.fori_loop(0, n_dom, one, 0)


def layer_kernel(
    n_dom, grid_x, grid_z,
    group_ref, block_ref, packed, feats_hbm, w_in, values_hbm, weights, masks,
    pushed, final,
    comb0, comb1, comb2, comb3, last, initial, feats, values, zs, zr, hs,
    load_sem, dom_send, dom_recv, z_send, z_recv, h_send, h_recv,
):
    comb = (comb0, comb1, comb2, comb3, last)
    f_me = lax.axis_index("feat")
    d_me = lax.axis_index("dom")
    x_me, z_me = d_me // grid_z, d_me % grid_z

    barrier = pltpu.get_barrier_semaphore()

    def greet_dom(i, carry):
        pl.semaphore_signal(
            barrier, inc=1, device_id=(f_me, lax.rem(d_me + 1 + i, n_dom)), device_id_type=MESH
        )
        return carry

    def greet_feat(i, carry):
        pl.semaphore_signal(
            barrier, inc=1, device_id=(lax.rem(f_me + 1 + i, NFEAT), d_me), device_id_type=MESH
        )
        return carry

    lax.fori_loop(0, n_dom - 1, greet_dom, 0)
    lax.fori_loop(0, NFEAT - 1, greet_feat, 0)
    load_feats = pltpu.make_async_copy(feats_hbm, feats, load_sem.at[0])
    load_values = pltpu.make_async_copy(values_hbm, values, load_sem.at[1])
    load_feats.start()
    load_values.start()
    pl.semaphore_wait(barrier, n_dom - 1 + NFEAT - 1)

    def dom_copy(level, k):
        i = lax.rem(k, grid_z)
        half = grid_z // 2
        dz = jnp.where(lax.rem(i, 2) == 1, half - (i + 1) // 2, half + i // 2)
        dx = lax.rem(grid_x - 1 - k // grid_z + i + 1, grid_x)
        dest = lax.rem(x_me + dx, grid_x) * grid_z + lax.rem(z_me + dz, grid_z)
        return pltpu.make_async_remote_copy(
            src_ref=packed.at[level, dest],
            dst_ref=comb[level].at[GROUPS + d_me],
            send_sem=dom_send.at[level, k],
            recv_sem=dom_recv.at[level, k],
            device_id=(f_me, dest),
            device_id_type=MESH,
        )

    def send_level(level):
        def one(k, carry):
            dom_copy(level, k).start()
            return carry

        lax.fori_loop(0, n_dom - 1, one, 0)

    def wait_level(level):
        def one(k, carry):
            dom_copy(level, k).wait_recv()
            return carry

        lax.fori_loop(0, n_dom - 1, one, 0)

    def feat_copy(source, target, send_sem, recv_sem, i):
        dest = lax.rem(f_me + 1 + i, NFEAT)
        return pltpu.make_async_remote_copy(
            src_ref=source.at[dest],
            dst_ref=target.at[f_me],
            send_sem=send_sem.at[i],
            recv_sem=recv_sem.at[i],
            device_id=(dest, d_me),
            device_id_type=MESH,
        )

    send_level(0)
    send_level(1)
    for level in range(LAYERS):
        comb[level][GROUPS + d_me] = jnp.zeros((TILE, LANES), BF)

    load_feats.wait()

    def start_group(g, carry):
        for c in range(2):
            rows = [
                feats[pl.ds(pl.multiple_of((g * PACK + t) * TILE + c * 64, 64), 64), :]
                for t in range(PACK)
            ]
            h0 = jnp.dot(jnp.concatenate(rows, axis=1), w_in[...], preferred_element_type=F32)
            h0 = jnp.maximum(h0, 0.0).astype(BF)
            comb0[g, pl.ds(c * 64, 64), :] = h0
            initial[g, pl.ds(c * 64, 64), :] = h0
        return carry

    lax.fori_loop(0, GROUPS, start_group, 0)
    load_values.wait()

    def emit_rows(level, target):
        def one(g, carry):
            flipped = comb[level][g].astype(F32).T.astype(BF)
            for t in range(PACK):
                start = pl.multiple_of((g * PACK + t) * TILE, TILE)
                target(flipped[t * WIDTH:(t + 1) * WIDTH], start)
            return carry

        lax.fori_loop(0, GROUPS, one, 0)

    for level in range(LAYERS):
        beta = math.log(LAMBDA_DECAY / (level + 1) + 1.0)
        wait_level(level)
        if level + 2 < LAYERS:
            send_level(level + 2)

        def propagate(i, carry):
            g = lax.rem(f_me + 1 + i, GROUPS)
            lane = lane_ids(TILE)
            agg = jnp.zeros((TILE, LANES), F32)
            for t in range(PACK):
                r = g * PACK + t
                picked = []
                for k in range(K):
                    tile = comb[level][group_ref[r, k]]
                    picked.append(tile * masks[block_ref[r, k]])
                lhs = jnp.concatenate([values[r, k] for k in range(K)], axis=1)
                out = jnp.dot(
                    lhs, jnp.concatenate(picked, axis=0), preferred_element_type=F32
                )
                out = out + pltpu.roll(out, 64, 1)
                out = out + pltpu.roll(out, 32, 1)
                agg = jnp.where((lane >> 5) == t, out, agg)
            z = (1.0 - ALPHA) * agg + ALPHA * initial[g].astype(F32)
            zs[level, g] = z.astype(BF)
            return carry

        def send_z(i):
            feat_copy(zs.at[level], zr.at[level], z_send.at[level], z_recv.at[level], i).start()

        def step(i, carry):
            propagate(i, 0)
            send_z(i - 1)
            return carry

        propagate(0, 0)
        lax.fori_loop(1, NFEAT, step, 0)
        zr[level, f_me] = zs[level, f_me]

        def push(part, start):
            pushed[level, :, pl.ds(start, TILE)] = part

        emit_rows(level, push)

        def wait_z(i, carry):
            feat_copy(
                zs.at[level], zr.at[level], z_send.at[level], z_recv.at[level], i
            ).wait_recv()
            return carry

        lax.fori_loop(0, NFEAT - 1, wait_z, 0)

        def mix(c, carry):
            start = pl.multiple_of(c * 32, 32)
            parts = [zr[level, f, pl.ds(start, 32), :].astype(F32) for f in range(NFEAT)]
            left = swap_blocks(parts[:4])
            right = swap_blocks(parts[4:])
            block = jnp.concatenate(
                [jnp.concatenate([left[t], right[t]], axis=1) for t in range(PACK)], axis=0
            )
            product = jnp.dot(block.astype(BF), weights[level], preferred_element_type=F32)
            fresh = jnp.maximum((1.0 - beta) * block + beta * product, 0.0)
            for a in range(2):
                outs = swap_blocks(
                    [fresh[t * 32:(t + 1) * 32, a * LANES:(a + 1) * LANES] for t in range(PACK)]
                )
                for b in range(PACK):
                    hs[level, a * PACK + b, pl.ds(start, 32), :] = outs[b].astype(BF)
            return carry

        lax.fori_loop(0, 4, mix, 0)
        comb[level + 1][f_me] = hs[level, f_me]

        def send_h(i, carry):
            feat_copy(
                hs.at[level], comb[level + 1], h_send.at[level], h_recv.at[level], i
            ).start()
            return carry

        def wait_h(i, carry):
            feat_copy(
                hs.at[level], comb[level + 1], h_send.at[level], h_recv.at[level], i
            ).wait_recv()
            return carry

        lax.fori_loop(0, NFEAT - 1, send_h, 0)
        lax.fori_loop(0, NFEAT - 1, wait_h, 0)

    def finish(part, start):
        final[:, pl.ds(start, TILE)] = part

    emit_rows(LAYERS, finish)

    for level in range(LAYERS):
        def drain_dom(k, carry):
            dom_copy(level, k).wait_send()
            return carry

        def drain_feat(i, carry):
            feat_copy(
                zs.at[level], zr.at[level], z_send.at[level], z_recv.at[level], i
            ).wait_send()
            feat_copy(
                hs.at[level], comb[level + 1], h_send.at[level], h_recv.at[level], i
            ).wait_send()
            return carry

        lax.fori_loop(0, n_dom - 1, drain_dom, 0)
        lax.fori_loop(0, NFEAT - 1, drain_feat, 0)


def on_device(
    n_dom, features, w_input, layer_weights, history, tile_values, tile_columns, send_rows, send_counts
):
    grid_x, grid_z = (4, 8) if n_dom == 32 else (1, n_dom)
    live = jnp.arange(CAP)[None, :] < send_counts[0][:, None]
    rows = jnp.where(live, send_rows[0], NODES_DEV)
    table_t = history.transpose(0, 2, 1).reshape(LAYERS * WIDTH, NODES_DEV)
    vmem = pl.BlockSpec(memory_space=pltpu.VMEM)
    smem = pl.BlockSpec(memory_space=pltpu.SMEM)
    hbm = pl.BlockSpec(memory_space=pl.ANY)
    packed = pl.pallas_call(
        functools.partial(gather_kernel, n_dom),
        out_shape=jax.ShapeDtypeStruct((LAYERS, n_dom, TILE, LANES), BF),
        in_specs=[smem, vmem],
        out_specs=vmem,
        scratch_shapes=[
            pltpu.VMEM((NODES_DEV + 8, LANES), F32),
            pltpu.VMEM((CAP, LANES), F32),
        ],
        name="gather_halo",
    )(rows, table_t)

    zero = jnp.zeros_like(w_input)
    w_in = jnp.concatenate(
        [
            jnp.concatenate([w_input if a == t else zero for a in range(PACK)], axis=1)
            for t in range(PACK)
        ],
        axis=0,
    )
    masks = (
        jnp.arange(LANES)[None, None, :] // WIDTH == jnp.arange(PACK)[:, None, None]
    ).astype(BF)
    masks = jnp.broadcast_to(masks, (PACK, TILE, LANES))
    sem = pltpu.SemaphoreType.DMA
    pushed, final = pl.pallas_call(
        functools.partial(layer_kernel, n_dom, grid_x, grid_z),
        out_shape=(
            jax.ShapeDtypeStruct((LAYERS, WIDTH, NODES_DEV), BF),
            jax.ShapeDtypeStruct((WIDTH, NODES_DEV), BF),
        ),
        in_specs=[smem, smem, hbm, hbm, vmem, hbm, vmem, vmem],
        out_specs=(vmem, vmem),
        scratch_shapes=[
            *[pltpu.VMEM((GROUPS + n_dom, TILE, LANES), BF) for _ in range(LAYERS)],
            pltpu.VMEM((GROUPS, TILE, LANES), BF),
            pltpu.VMEM((GROUPS, TILE, LANES), BF),
            pltpu.VMEM((NODES_DEV, LANES), BF),
            pltpu.VMEM((NODES_DEV // TILE, K, TILE, TILE), BF),
            pltpu.VMEM((LAYERS, NFEAT, TILE, LANES), BF),
            pltpu.VMEM((LAYERS, NFEAT, TILE, LANES), BF),
            pltpu.VMEM((LAYERS, NFEAT, TILE, LANES), BF),
            sem((2,)),
            sem((LAYERS, n_dom - 1)),
            sem((LAYERS, n_dom - 1)),
            sem((LAYERS, NFEAT - 1)),
            sem((LAYERS, NFEAT - 1)),
            sem((LAYERS, NFEAT - 1)),
            sem((LAYERS, NFEAT - 1)),
        ],
        compiler_params=pltpu.CompilerParams(collective_id=0, has_side_effects=True),
        name="halo_layers",
    )(
        tile_columns // PACK, tile_columns % PACK, packed, features, w_in, tile_values,
        layer_weights, masks,
    )
    return pushed.transpose(0, 2, 1), final.transpose(1, 0)


def solution(mesh):
    placed = (
        P("dom", None),
        P(None, "feat"),
        P(),
        P(None, "dom", "feat"),
        P("dom", None, None, None),
        P("dom", None),
        P("dom", None, None),
        P("dom", None),
    )
    return jax.shard_map(
        functools.partial(on_device, mesh.shape["dom"]),
        mesh=mesh,
        in_specs=placed,
        out_specs=(P(None, "dom", "feat"), P("dom", "feat")),
        check_vma=False,
    )
```

time: 481 us -> 167 us (0.35)
  local copies, waits for them, and re-layouts: 230 us -> 6.22 us
  Pallas kernels: 0 us -> 157 us
  waiting for transfers between devices: 123 us -> 0 us
  matrix products: 39.6 us -> 0 us
  blocking collectives: 36.4 us -> 0 us
  starting transfers between devices: 33.9 us -> 0 us
  other arithmetic: 15.2 us -> 2.96 us
    pallas_call x0 -> x2, Pallas kernels: none -> 157 us  [the longest x1 126 us: on_device(): pl.pallas_call(functools.partial(layer_kernel, n_dom, grid_x, grid_z), ou...]
    gather x2 -> x0, local copies, waits for them, and re-layouts: 136 us -> none  [on_device(): packed = jnp.where(live_slots[None], history[:, targets], zero_value)]
    all_to_all x6 -> x0, waiting for transfers between devices: 123 us -> none  [the longest x1 91.9 us: on_device(): lax.all_to_all(packed, 'dom', split_axis=1, concat_axis=1, tiled=True)]
    reshape x12 -> x0, local copies, waits for them, and re-layouts: 57.7 us -> none  [the longest x4 32 us: propagate(): flat_tiles = combined.reshape(tile_count, tile_size * slice_width)]
    dot_general x13 -> x0, matrix products: 39.6 us -> none  [the longest x4 26.8 us: propagate(): jnp.einsum('rkab,rkbf->raf', values, picked, preferred_element_type=jnp.f...]
    all_to_all x3 -> x0, blocking collectives: 36.4 us -> none  [on_device(): lax.all_to_all(stacked, 'feat', split_axis=0, concat_axis=2, tiled=True)[0]]
    all_to_all x6 -> x0, starting transfers between devices: 33.9 us -> none  [the longest x4 17.4 us: on_device(): lax.all_to_all(fresh.astype(jnp.bfloat16)[None], 'feat', split_axis=2, co...]
    concatenate x4 -> x0, local copies, waits for them, and re-layouts: 16.1 us -> none  [propagate(): combined = jnp.concatenate([own_rows, halo_rows], axis=0)]
  transfers between devices with their start and end apart: 6 -> 0, of which waited for: 6 -> 0; matrix products, arithmetic and copies ran while one was open for 0% -> 0% of each run, Pallas kernels for 0% -> 0%
where the time goes in v1:
time: 167 us
  Pallas kernels  157 us (94%)
  local copies, waits for them, and re-layouts  6.22 us (4%)
  other arithmetic  2.96 us (2%)
    pallas_call x1, Pallas kernels, on_device(): pl.pallas_call(functools.partial(layer_kernel, n_dom, grid_x, grid_z), ou...  126 us
    pallas_call x1, Pallas kernels, on_device(): pl.pallas_call(functools.partial(gather_kernel, n_dom), out_shape=jax.Sha...  31 us
    unnamed x4, local copies, waits for them, and re-layouts  5.53 us

profile of v1, /device:TPU:1, one launch (start us, length us, event | category | flops | bytes accessed | tf_op | source)
XLA Modules:
  0.0 167.1 jit_solution(15535216832667579603)
XLA Ops:
  0.7 0.8 copy.10
  1.4 0.6 add_select_fusion
  2.1 0.8 copy.14
  2.9 0.8 fusion.2.w_in
  3.7 1.5 bitcast_select_fusion.rows
  5.2 0.7 broadcast_in_dim.17.masks
  5.9 31.0 %gather_halo.1.packed = bf16[4,32,128,128]{3,2,1,0:T(8,128)(2,1)} custom-call(s32[32,512]{1,0:T(8,128)} %bitcast_select_fusion.rows, bf16[128,4096]{1,0:T(8,128)(2,1)} %bitcast.9), custom_call_target="tpu_custom_call" | custom-call | tf_op jit(solution)/shard_map/gather_halo/pallas_call | solution.py:310
  36.9 126.3 %halo_layers.1 = (bf16[4,32,4096]{2,1,0:T(8,128)(2,1)}, bf16[32,4096]{1,0:T(8,128)(2,1)}) custom-call(s32[32,6]{1,0:T(8,128)} %get-tuple-element.7.group_ref, s32[32,6]{1,0:T(8,128)} %get-tuple-element.6.block_ref, bf16[4,32,128,128]{3,2,1,0:T(8,128)(2,1)} %gather_halo.1.packed, bf16[4096,128]{1,0:T(8,128)(2,1)} %feats_hbm.1, bf16[512,128]{1,0:T(8,128)(2,1)} %fusion.2.w_in, ...), custom_call_target="tpu_custom_call" | custom-call | tf_op jit(solution)/shard_map/halo_layers/pallas_call | solution.py:335
  163.2 2.3 %copy.20 = bf16[4,4096,32]{1,2,0:T(8,128)(2,1)} copy(bf16[4,4096,32]{1,2,0:T(8,128)(2,1)} %bitcast.8) | data formatting | bytes 2097152
  165.5 1.7 copy.21
  (4 shorter events, 0.0 us)

commit v2 on v1

--- a/solution.py
+++ b/solution.py
@@ -49,42 +49,37 @@
 def fill_table(table_t, table):
     def block(i, carry):
         start = pl.multiple_of(i * TILE, TILE)
-        part = table_t[:, pl.ds(start, TILE)].astype(F32)
-        table[pl.ds(start, TILE), :] = part.T
+        table[pl.ds(start, TILE), :] = table_t[:, pl.ds(start, TILE)].astype(F32).T
         return carry
 
     lax.fori_loop(0, NODES_DEV // TILE, block, 0)
-    table[pl.ds(NODES_DEV, 8), :] = jnp.zeros((8, LANES), F32)
 
 
 def gather_rows(rows, table, picked, dest):
+    base = dest * CAP
     for j in range(CAP):
-        picked[pl.ds(j, 1), :] = table[pl.ds(rows[dest, j], 1), :]
-
-
-def pack_rows(picked, packed, dest):
+        picked[pl.ds(j, 1), :] = table[pl.ds(rows[base + j], 1), :]
+
+
+def pack_rows(counts, picked, packed, dest):
+    row = lax.broadcasted_iota(jnp.int32, (32, LANES), 0)
+    count = counts[0, dest]
     for c in range(4):
-        parts = [picked[pl.ds(t * TILE + c * 32, 32), :] for t in range(PACK)]
+        parts = []
+        for t in range(PACK):
+            start = t * TILE + c * 32
+            live = row < count - start
+            parts.append(jnp.where(live, picked[pl.ds(start, 32), :], 0.0))
         for level, part in enumerate(swap_blocks(parts)):
             packed[level, dest, pl.ds(c * 32, 32), :] = part.astype(BF)
 
 
-def gather_kernel(n_dom, rows, table_t, packed, table, picked):
-    fill_table(table_t, table)
-
-    def one(dest, carry):
-        gather_rows(rows, table, picked, dest)
-        pack_rows(picked, packed, dest)
-        return carry
-
-    lax.fori_loop(0, n_dom, one, 0)
-
-
 def layer_kernel(
     n_dom, grid_x, grid_z,
-    group_ref, block_ref, packed, feats_hbm, w_in, values_hbm, weights, masks,
+    columns, rows, counts, table_hbm, feats_hbm, w_in_t, values_hbm, weights_hbm,
     pushed, final,
-    comb0, comb1, comb2, comb3, last, initial, feats, values, zs, zr, hs,
+    table_t, table, picked, packed, masks, w_wide,
+    comb0, comb1, comb2, comb3, last, initial, feats, values, weights, zs, zr, hs,
     load_sem, dom_send, dom_recv, z_send, z_recv, h_send, h_recv,
 ):
     comb = (comb0, comb1, comb2, comb3, last)
@@ -108,18 +103,33 @@
 
     lax.fori_loop(0, n_dom - 1, greet_dom, 0)
     lax.fori_loop(0, NFEAT - 1, greet_feat, 0)
-    load_feats = pltpu.make_async_copy(feats_hbm, feats, load_sem.at[0])
-    load_values = pltpu.make_async_copy(values_hbm, values, load_sem.at[1])
+    load_table = pltpu.make_async_copy(table_hbm, table_t, load_sem.at[0])
+    load_feats = pltpu.make_async_copy(feats_hbm, feats, load_sem.at[1])
+    load_values = pltpu.make_async_copy(values_hbm, values, load_sem.at[2])
+    load_weights = pltpu.make_async_copy(weights_hbm, weights, load_sem.at[3])
+    load_table.start()
     load_feats.start()
     load_values.start()
+    load_weights.start()
+    lane = lane_ids(TILE)
+    for b in range(PACK):
+        masks[b] = jnp.where((lane >> 5) == b, 1.0, 0.0).astype(BF)
+    w_wide[...] = jnp.zeros((LANES, PACK * TILE), BF)
+    for t in range(PACK):
+        w_wide[t * WIDTH:(t + 1) * WIDTH, t * TILE:(t + 1) * TILE] = w_in_t[...]
+    load_table.wait()
+    fill_table(table_t, table)
     pl.semaphore_wait(barrier, n_dom - 1 + NFEAT - 1)
 
-    def dom_copy(level, k):
+    def dest_of(k):
         i = lax.rem(k, grid_z)
         half = grid_z // 2
         dz = jnp.where(lax.rem(i, 2) == 1, half - (i + 1) // 2, half + i // 2)
         dx = lax.rem(grid_x - 1 - k // grid_z + i + 1, grid_x)
-        dest = lax.rem(x_me + dx, grid_x) * grid_z + lax.rem(z_me + dz, grid_z)
+        return lax.rem(x_me + dx, grid_x) * grid_z + lax.rem(z_me + dz, grid_z)
+
+    def dom_copy(level, k):
+        dest = dest_of(k)
         return pltpu.make_async_remote_copy(
             src_ref=packed.at[level, dest],
             dst_ref=comb[level].at[GROUPS + d_me],
@@ -154,20 +164,36 @@
             device_id_type=MESH,
         )
 
-    send_level(0)
-    send_level(1)
+    def gather(k, carry):
+        dest = dest_of(k)
+        gather_rows(rows, table, picked, dest)
+        pack_rows(counts, picked, packed, dest)
+        return carry
+
+    def gather_step(k, carry):
+        gather(k, 0)
+        dom_copy(0, k - 1).start()
+        return carry
+
+    gather(0, 0)
+    lax.fori_loop(1, n_dom - 1, gather_step, 0)
     for level in range(LAYERS):
         comb[level][GROUPS + d_me] = jnp.zeros((TILE, LANES), BF)
 
+    dom_copy(0, n_dom - 2).start()
+    send_level(1)
     load_feats.wait()
 
     def start_group(g, carry):
         for c in range(2):
-            rows = [
+            own = [
                 feats[pl.ds(pl.multiple_of((g * PACK + t) * TILE + c * 64, 64), 64), :]
                 for t in range(PACK)
             ]
-            h0 = jnp.dot(jnp.concatenate(rows, axis=1), w_in[...], preferred_element_type=F32)
+            h0 = lax.dot_general(
+                jnp.concatenate(own, axis=1), w_wide[...], (((1,), (1,)), ((), ())),
+                preferred_element_type=F32,
+            )
             h0 = jnp.maximum(h0, 0.0).astype(BF)
             comb0[g, pl.ds(c * 64, 64), :] = h0
             initial[g, pl.ds(c * 64, 64), :] = h0
@@ -175,6 +201,7 @@
 
     lax.fori_loop(0, GROUPS, start_group, 0)
     load_values.wait()
+    load_weights.wait()
 
     def emit_rows(level, target):
         def one(g, carry):
@@ -198,13 +225,13 @@
             agg = jnp.zeros((TILE, LANES), F32)
             for t in range(PACK):
                 r = g * PACK + t
-                picked = []
+                tiles = []
                 for k in range(K):
-                    tile = comb[level][group_ref[r, k]]
-                    picked.append(tile * masks[block_ref[r, k]])
+                    column = columns[k, r]
+                    tiles.append(comb[level][column >> 2] * masks[column & 3])
                 lhs = jnp.concatenate([values[r, k] for k in range(K)], axis=1)
                 out = jnp.dot(
-                    lhs, jnp.concatenate(picked, axis=0), preferred_element_type=F32
+                    lhs, jnp.concatenate(tiles, axis=0), preferred_element_type=F32
                 )
                 out = out + pltpu.roll(out, 64, 1)
                 out = out + pltpu.roll(out, 32, 1)
@@ -301,36 +328,10 @@
     n_dom, features, w_input, layer_weights, history, tile_values, tile_columns, send_rows, send_counts
 ):
     grid_x, grid_z = (4, 8) if n_dom == 32 else (1, n_dom)
-    live = jnp.arange(CAP)[None, :] < send_counts[0][:, None]
-    rows = jnp.where(live, send_rows[0], NODES_DEV)
     table_t = history.transpose(0, 2, 1).reshape(LAYERS * WIDTH, NODES_DEV)
     vmem = pl.BlockSpec(memory_space=pltpu.VMEM)
     smem = pl.BlockSpec(memory_space=pltpu.SMEM)
     hbm = pl.BlockSpec(memory_space=pl.ANY)
-    packed = pl.pallas_call(
-        functools.partial(gather_kernel, n_dom),
-        out_shape=jax.ShapeDtypeStruct((LAYERS, n_dom, TILE, LANES), BF),
-        in_specs=[smem, vmem],
-        out_specs=vmem,
-        scratch_shapes=[
-            pltpu.VMEM((NODES_DEV + 8, LANES), F32),
-            pltpu.VMEM((CAP, LANES), F32),
-        ],
-        name="gather_halo",
-    )(rows, table_t)
-
-    zero = jnp.zeros_like(w_input)
-    w_in = jnp.concatenate(
-        [
-            jnp.concatenate([w_input if a == t else zero for a in range(PACK)], axis=1)
-            for t in range(PACK)
-        ],
-        axis=0,
-    )
-    masks = (
-        jnp.arange(LANES)[None, None, :] // WIDTH == jnp.arange(PACK)[:, None, None]
-    ).astype(BF)
-    masks = jnp.broadcast_to(masks, (PACK, TILE, LANES))
     sem = pltpu.SemaphoreType.DMA
     pushed, final = pl.pallas_call(
         functools.partial(layer_kernel, n_dom, grid_x, grid_z),
@@ -338,18 +339,25 @@
             jax.ShapeDtypeStruct((LAYERS, WIDTH, NODES_DEV), BF),
             jax.ShapeDtypeStruct((WIDTH, NODES_DEV), BF),
         ),
-        in_specs=[smem, smem, hbm, hbm, vmem, hbm, vmem, vmem],
+        in_specs=[smem, smem, smem, hbm, hbm, vmem, hbm, hbm],
         out_specs=(vmem, vmem),
         scratch_shapes=[
+            pltpu.VMEM((LAYERS * WIDTH, NODES_DEV), BF),
+            pltpu.VMEM((NODES_DEV, LANES), F32),
+            pltpu.VMEM((CAP, LANES), F32),
+            pltpu.VMEM((LAYERS, n_dom, TILE, LANES), BF),
+            pltpu.VMEM((PACK, TILE, LANES), BF),
+            pltpu.VMEM((LANES, PACK * TILE), BF),
             *[pltpu.VMEM((GROUPS + n_dom, TILE, LANES), BF) for _ in range(LAYERS)],
             pltpu.VMEM((GROUPS, TILE, LANES), BF),
             pltpu.VMEM((GROUPS, TILE, LANES), BF),
             pltpu.VMEM((NODES_DEV, LANES), BF),
             pltpu.VMEM((NODES_DEV // TILE, K, TILE, TILE), BF),
+            pltpu.VMEM((LAYERS, F, F), BF),
             pltpu.VMEM((LAYERS, NFEAT, TILE, LANES), BF),
             pltpu.VMEM((LAYERS, NFEAT, TILE, LANES), BF),
             pltpu.VMEM((LAYERS, NFEAT, TILE, LANES), BF),
-            sem((2,)),
+            sem((4,)),
             sem((LAYERS, n_dom - 1)),
             sem((LAYERS, n_dom - 1)),
             sem((LAYERS, NFEAT - 1)),
@@ -360,8 +368,8 @@
         compiler_params=pltpu.CompilerParams(collective_id=0, has_side_effects=True),
         name="halo_layers",
     )(
-        tile_columns // PACK, tile_columns % PACK, packed, features, w_in, tile_values,
-        layer_weights, masks,
+        tile_columns.T, send_rows.reshape(-1), send_counts, table_t, features, w_input.T,
+        tile_values, layer_weights,
     )
     return pushed.transpose(0, 2, 1), final.transpose(1, 0)
 

time: 167 us -> 137 us (0.82)
  Pallas kernels: 157 us -> 131 us
  other arithmetic: 2.96 us -> 0 us
    pallas_call x1 -> x0, Pallas kernels: 31 us -> none  [on_device(): pl.pallas_call(functools.partial(gather_kernel, n_dom), out_shape=jax.Sha...]
    pallas_call x1, Pallas kernels: 126 us -> 131 us  [on_device(): pl.pallas_call(functools.partial(layer_kernel, n_dom, grid_x, grid_z), ou...]
    select_n x3 -> x0, other arithmetic: 2.18 us -> none  [the longest x1 1.55 us: on_device(): rows = jnp.where(live, send_rows[0], NODES_DEV)]
    unnamed x4 -> x3, local copies, waits for them, and re-layouts: 5.53 us -> 5.44 us
where the time goes in v2:
time: 137 us
  Pallas kernels  131 us (96%)
  local copies, waits for them, and re-layouts  5.44 us (4%)
    pallas_call x1, Pallas kernels, on_device(): pl.pallas_call(functools.partial(layer_kernel, n_dom, grid_x, grid_z), ou...  131 us
    unnamed x3, local copies, waits for them, and re-layouts  5.44 us

profile of v2, /device:TPU:1, one launch (start us, length us, event | category | flops | bytes accessed | tf_op | source)
XLA Modules:
  0.0 136.6 jit_solution(12988349481948901029)
XLA Ops:
  0.6 1.5 %copy.10 = s32[4,4,8,128]{3,1,2,0:T(4,128)} copy(s32[4,4,8,128]{3,2,1,0:T(8,128)} %bitcast.13) | data formatting | bytes 131072
  2.1 130.5 %halo_layers.1 = (bf16[4,32,4096]{2,1,0:T(8,128)(2,1)}, bf16[32,4096]{1,0:T(8,128)(2,1)}) custom-call(s32[6,32]{1,0:T(8,128)} %bitcast.15, s32[16384]{0:T(1024)} %bitcast.11, s32[1,32]{1,0:T(1,128)} %counts.1, bf16[128,4096]{1,0:T(8,128)(2,1)} %bitcast.9, bf16[4096,128]{1,0:T(8,128)(2,1)} %feats_hbm.1, bf16[32,128]{1,0:T(8,128)(2,1)} %bitcast.14, ...), custom_call_target="tpu_custom_call" | custom-call | tf_op jit(solution)/shard_map/halo_layers/pallas_call | solution.py:336
  132.6 2.3 %copy.13 = bf16[4,4096,32]{1,2,0:T(8,128)(2,1)} copy(bf16[4,4096,32]{1,2,0:T(8,128)(2,1)} %bitcast.10) | data formatting | bytes 2097152
  134.9 1.7 %copy.14 = bf16[4096,32]{0,1:T(8,128)(2,1)} copy(bf16[4096,32]{0,1:T(8,128)(2,1)} %bitcast.12) | data formatting | bytes 524288

commit v3 on v2

--- a/solution.py
+++ b/solution.py
@@ -13,6 +13,7 @@
 ALPHA = 0.1
 LAMBDA_DECAY = 0.5
 TILE = 128
+HALF = 64
 LANES = 128
 PACK = 4
 WIDTH = 32
@@ -49,16 +50,17 @@
 def fill_table(table_t, table):
     def block(i, carry):
         start = pl.multiple_of(i * TILE, TILE)
-        table[pl.ds(start, TILE), :] = table_t[:, pl.ds(start, TILE)].astype(F32).T
+        table[pl.ds(start, TILE), :] = table_t[:, pl.ds(start, TILE)].T.astype(F32)
         return carry
 
     lax.fori_loop(0, NODES_DEV // TILE, block, 0)
 
 
 def gather_rows(rows, table, picked, dest):
-    base = dest * CAP
-    for j in range(CAP):
-        picked[pl.ds(j, 1), :] = table[pl.ds(rows[base + j], 1), :]
+    high, low = dest // 8, dest % 8
+    for t in range(PACK):
+        for i in range(TILE):
+            picked[pl.ds(t * TILE + i, 1), :] = table[pl.ds(rows[high, t, low, i], 1), :]
 
 
 def pack_rows(counts, picked, packed, dest):
@@ -95,9 +97,16 @@
         )
         return carry
 
+    def feat_peer(i, sign):
+        pair, odd = i // 2, lax.rem(i, 2)
+        step = jnp.where(pair == 0, 2, jnp.where(pair == 1, 1, jnp.where(pair == 2, 3, 0)))
+        flip = jnp.where(pair == 3, 1 - odd, odd)
+        chip = lax.rem(f_me // 2 + 4 + sign * step, 4)
+        return chip * 2 + lax.rem(f_me + flip, 2)
+
     def greet_feat(i, carry):
         pl.semaphore_signal(
-            barrier, inc=1, device_id=(lax.rem(f_me + 1 + i, NFEAT), d_me), device_id_type=MESH
+            barrier, inc=1, device_id=(feat_peer(i, 1), d_me), device_id_type=MESH
         )
         return carry
 
@@ -153,13 +162,25 @@
 
         lax.fori_loop(0, n_dom - 1, one, 0)
 
-    def feat_copy(source, target, send_sem, recv_sem, i):
-        dest = lax.rem(f_me + 1 + i, NFEAT)
+    def z_copy(level, i):
+        dest = feat_peer(i, 1)
         return pltpu.make_async_remote_copy(
-            src_ref=source.at[dest],
-            dst_ref=target.at[f_me],
-            send_sem=send_sem.at[i],
-            recv_sem=recv_sem.at[i],
+            src_ref=zs.at[level, dest],
+            dst_ref=zr.at[level, f_me],
+            send_sem=z_send.at[level, i],
+            recv_sem=z_recv.at[level, i],
+            device_id=(dest, d_me),
+            device_id_type=MESH,
+        )
+
+    def h_copy(level, half, i):
+        dest = feat_peer(i, 1)
+        part = pl.ds(pl.multiple_of(half * HALF, HALF), HALF)
+        return pltpu.make_async_remote_copy(
+            src_ref=hs.at[level, dest, part],
+            dst_ref=comb[level + 1].at[f_me, part],
+            send_sem=h_send.at[level, half, i],
+            recv_sem=h_recv.at[level, half, i],
             device_id=(dest, d_me),
             device_id_type=MESH,
         )
@@ -203,15 +224,11 @@
     load_values.wait()
     load_weights.wait()
 
-    def emit_rows(level, target):
-        def one(g, carry):
-            flipped = comb[level][g].astype(F32).T.astype(BF)
-            for t in range(PACK):
-                start = pl.multiple_of((g * PACK + t) * TILE, TILE)
-                target(flipped[t * WIDTH:(t + 1) * WIDTH], start)
-            return carry
-
-        lax.fori_loop(0, GROUPS, one, 0)
+    def emit_group(level, g, target):
+        flipped = comb[level][g].T
+        for t in range(PACK):
+            start = pl.multiple_of((g * PACK + t) * TILE, TILE)
+            target(flipped[t * WIDTH:(t + 1) * WIDTH], start)
 
     for level in range(LAYERS):
         beta = math.log(LAMBDA_DECAY / (level + 1) + 1.0)
@@ -220,7 +237,7 @@
             send_level(level + 2)
 
         def propagate(i, carry):
-            g = lax.rem(f_me + 1 + i, GROUPS)
+            g = feat_peer(i, 1)
             lane = lane_ids(TILE)
             agg = jnp.zeros((TILE, LANES), F32)
             for t in range(PACK):
@@ -240,12 +257,9 @@
             zs[level, g] = z.astype(BF)
             return carry
 
-        def send_z(i):
-            feat_copy(zs.at[level], zr.at[level], z_send.at[level], z_recv.at[level], i).start()
-
         def step(i, carry):
             propagate(i, 0)
-            send_z(i - 1)
+            z_copy(level, i - 1).start()
             return carry
 
         propagate(0, 0)
@@ -255,18 +269,20 @@
         def push(part, start):
             pushed[level, :, pl.ds(start, TILE)] = part
 
-        emit_rows(level, push)
+        def push_group(g, carry):
+            emit_group(level, g, push)
+            return carry
+
+        lax.fori_loop(0, GROUPS, push_group, 0)
 
         def wait_z(i, carry):
-            feat_copy(
-                zs.at[level], zr.at[level], z_send.at[level], z_recv.at[level], i
-            ).wait_recv()
+            z_copy(level, i).wait_recv()
             return carry
 
         lax.fori_loop(0, NFEAT - 1, wait_z, 0)
 
-        def mix(c, carry):
-            start = pl.multiple_of(c * 32, 32)
+        def mix(half, piece):
+            start = pl.multiple_of(half * HALF + piece * 32, 32)
             parts = [zr[level, f, pl.ds(start, 32), :].astype(F32) for f in range(NFEAT)]
             left = swap_blocks(parts[:4])
             right = swap_blocks(parts[4:])
@@ -281,30 +297,39 @@
                 )
                 for b in range(PACK):
                     hs[level, a * PACK + b, pl.ds(start, 32), :] = outs[b].astype(BF)
-            return carry
-
-        lax.fori_loop(0, 4, mix, 0)
+
+        def mix_half(half, carry):
+            mix(half, 0)
+            mix(half, 1)
+
+            def send_h(i, inner):
+                h_copy(level, half, i).start()
+                return inner
+
+            lax.fori_loop(0, NFEAT - 1, send_h, 0)
+            return carry
+
+        lax.fori_loop(0, 2, mix_half, 0)
         comb[level + 1][f_me] = hs[level, f_me]
 
-        def send_h(i, carry):
-            feat_copy(
-                hs.at[level], comb[level + 1], h_send.at[level], h_recv.at[level], i
-            ).start()
-            return carry
-
         def wait_h(i, carry):
-            feat_copy(
-                hs.at[level], comb[level + 1], h_send.at[level], h_recv.at[level], i
-            ).wait_recv()
-            return carry
-
-        lax.fori_loop(0, NFEAT - 1, send_h, 0)
-        lax.fori_loop(0, NFEAT - 1, wait_h, 0)
+            h_copy(level, 0, i).wait_recv()
+            h_copy(level, 1, i).wait_recv()
+            return carry
+
+        if level + 1 < LAYERS:
+            lax.fori_loop(0, NFEAT - 1, wait_h, 0)
 
     def finish(part, start):
         final[:, pl.ds(start, TILE)] = part
 
-    emit_rows(LAYERS, finish)
+    def finish_group(i, carry):
+        wait_h(i, 0)
+        emit_group(LAYERS, feat_peer(i, -1), finish)
+        return carry
+
+    emit_group(LAYERS, f_me, finish)
+    lax.fori_loop(0, NFEAT - 1, finish_group, 0)
 
     for level in range(LAYERS):
         def drain_dom(k, carry):
@@ -312,12 +337,9 @@
             return carry
 
         def drain_feat(i, carry):
-            feat_copy(
-                zs.at[level], zr.at[level], z_send.at[level], z_recv.at[level], i
-            ).wait_send()
-            feat_copy(
-                hs.at[level], comb[level + 1], h_send.at[level], h_recv.at[level], i
-            ).wait_send()
+            z_copy(level, i).wait_send()
+            h_copy(level, 0, i).wait_send()
+            h_copy(level, 1, i).wait_send()
             return carry
 
         lax.fori_loop(0, n_dom - 1, drain_dom, 0)
@@ -336,8 +358,8 @@
     pushed, final = pl.pallas_call(
         functools.partial(layer_kernel, n_dom, grid_x, grid_z),
         out_shape=(
-            jax.ShapeDtypeStruct((LAYERS, WIDTH, NODES_DEV), BF),
-            jax.ShapeDtypeStruct((WIDTH, NODES_DEV), BF),
+            pltpu.VMEM((LAYERS, WIDTH, NODES_DEV), BF),
+            pltpu.VMEM((WIDTH, NODES_DEV), BF),
         ),
         in_specs=[smem, smem, smem, hbm, hbm, vmem, hbm, hbm],
         out_specs=(vmem, vmem),
@@ -362,13 +384,13 @@
             sem((LAYERS, n_dom - 1)),
             sem((LAYERS, NFEAT - 1)),
             sem((LAYERS, NFEAT - 1)),
-            sem((LAYERS, NFEAT - 1)),
-            sem((LAYERS, NFEAT - 1)),
+            sem((LAYERS, 2, NFEAT - 1)),
+            sem((LAYERS, 2, NFEAT - 1)),
         ],
         compiler_params=pltpu.CompilerParams(collective_id=0, has_side_effects=True),
         name="halo_layers",
     )(
-        tile_columns.T, send_rows.reshape(-1), send_counts, table_t, features, w_input.T,
+        tile_columns.T, send_rows.reshape(n_dom // 8, 8, PACK, TILE).transpose(0, 2, 1, 3), send_counts, table_t, features, w_input.T,
         tile_values, layer_weights,
     )
     return pushed.transpose(0, 2, 1), final.transpose(1, 0)

time: 137 us -> 129 us (0.942)
  Pallas kernels: 131 us -> 127 us
  local copies, waits for them, and re-layouts: 5.44 us -> 1.67 us
    unnamed x3 -> x2, local copies, waits for them, and re-layouts: 5.44 us -> 1.67 us
    pallas_call x1, Pallas kernels: 131 us -> 127 us  [on_device(): pl.pallas_call(functools.partial(layer_kernel, n_dom, grid_x, grid_z), ou...]
where the time goes in v3:
time: 129 us
  Pallas kernels  127 us (98%)
  local copies, waits for them, and re-layouts  1.67 us (1%)
    pallas_call x1, Pallas kernels, on_device(): pl.pallas_call(functools.partial(layer_kernel, n_dom, grid_x, grid_z), ou...  127 us

profile of v3, /device:TPU:1, one launch (start us, length us, event | category | flops | bytes accessed | tf_op | source)
XLA Modules:
  0.0 129.2 jit_solution(8434075114877836590)
XLA Ops:
  0.6 126.8 %halo_layers.1 = (bf16[4,32,4096]{2,1,0:T(8,128)(2,1)S(1)}, bf16[32,4096]{1,0:T(8,128)(2,1)S(1)}) custom-call(s32[6,32]{1,0:T(8,128)} %bitcast.15, s32[4,4,8,128]{3,2,1,0:T(8,128)} %bitcast.13, s32[1,32]{1,0:T(1,128)} %counts.1, bf16[128,4096]{1,0:T(8,128)(2,1)} %bitcast.12, bf16[4096,128]{1,0:T(8,128)(2,1)} %feats_hbm.1, bf16[32,128]{1,0:T(8,128)(2,1)} %bitcast.14, ...), custom_call_target="tpu_custom_call" | custom-call | tf_op jit(solution)/shard_map/halo_layers/pallas_call | solution.py:358
  127.5 1.0 copy.12
  128.5 0.7 copy.13

commit v4 on v3

--- a/solution.py
+++ b/solution.py
@@ -47,13 +47,14 @@
     return y0, y1, y2, y3
 
 
-def fill_table(table_t, table):
+def fill_table(table_t, table, piece):
     def block(i, carry):
-        start = pl.multiple_of(i * TILE, TILE)
-        table[pl.ds(start, TILE), :] = table_t[:, pl.ds(start, TILE)].T.astype(F32)
-        return carry
-
-    lax.fori_loop(0, NODES_DEV // TILE, block, 0)
+        for u in range(4):
+            start = pl.multiple_of((piece * 8 + i * 4 + u) * TILE, TILE)
+            table[pl.ds(start, TILE), :] = table_t[:, pl.ds(start, TILE)].T.astype(F32)
+        return carry
+
+    lax.fori_loop(0, 2, block, 0)
 
 
 def gather_rows(rows, table, picked, dest):
@@ -82,12 +83,21 @@
     pushed, final,
     table_t, table, picked, packed, masks, w_wide,
     comb0, comb1, comb2, comb3, last, initial, feats, values, weights, zs, zr, hs,
-    load_sem, dom_send, dom_recv, z_send, z_recv, h_send, h_recv,
+    table_sem, load_sem, dom_send, dom_recv, z_send, z_recv, h_send, h_recv,
 ):
     comb = (comb0, comb1, comb2, comb3, last)
     f_me = lax.axis_index("feat")
     d_me = lax.axis_index("dom")
     x_me, z_me = d_me // grid_z, d_me % grid_z
+
+    def load_table(piece):
+        part = pl.ds(piece * (NODES_DEV // 4), NODES_DEV // 4)
+        return pltpu.make_async_copy(
+            table_hbm.at[:, part], table_t.at[:, part], table_sem.at[piece]
+        )
+
+    for piece in range(4):
+        load_table(piece).start()
 
     barrier = pltpu.get_barrier_semaphore()
 
@@ -112,11 +122,9 @@
 
     lax.fori_loop(0, n_dom - 1, greet_dom, 0)
     lax.fori_loop(0, NFEAT - 1, greet_feat, 0)
-    load_table = pltpu.make_async_copy(table_hbm, table_t, load_sem.at[0])
     load_feats = pltpu.make_async_copy(feats_hbm, feats, load_sem.at[1])
     load_values = pltpu.make_async_copy(values_hbm, values, load_sem.at[2])
     load_weights = pltpu.make_async_copy(weights_hbm, weights, load_sem.at[3])
-    load_table.start()
     load_feats.start()
     load_values.start()
     load_weights.start()
@@ -126,9 +134,9 @@
     w_wide[...] = jnp.zeros((LANES, PACK * TILE), BF)
     for t in range(PACK):
         w_wide[t * WIDTH:(t + 1) * WIDTH, t * TILE:(t + 1) * TILE] = w_in_t[...]
-    load_table.wait()
-    fill_table(table_t, table)
-    pl.semaphore_wait(barrier, n_dom - 1 + NFEAT - 1)
+    for piece in range(4):
+        load_table(piece).wait()
+        fill_table(table_t, table, piece)
 
     def dest_of(k):
         i = lax.rem(k, grid_z)
@@ -196,8 +204,15 @@
         dom_copy(0, k - 1).start()
         return carry
 
-    gather(0, 0)
-    lax.fori_loop(1, n_dom - 1, gather_step, 0)
+    def send_first(k, carry):
+        dom_copy(0, k).start()
+        return carry
+
+    ahead = min(2, n_dom - 1)
+    lax.fori_loop(0, ahead, gather, 0)
+    pl.semaphore_wait(barrier, n_dom - 1 + NFEAT - 1)
+    lax.fori_loop(0, ahead - 1, send_first, 0)
+    lax.fori_loop(ahead, n_dom - 1, gather_step, 0)
     for level in range(LAYERS):
         comb[level][GROUPS + d_me] = jnp.zeros((TILE, LANES), BF)
 
@@ -229,6 +244,11 @@
         for t in range(PACK):
             start = pl.multiple_of((g * PACK + t) * TILE, TILE)
             target(flipped[t * WIDTH:(t + 1) * WIDTH], start)
+
+    def drain_h(level, i, carry):
+        h_copy(level, 0, i).wait_send()
+        h_copy(level, 1, i).wait_send()
+        return carry
 
     for level in range(LAYERS):
         beta = math.log(LAMBDA_DECAY / (level + 1) + 1.0)
@@ -312,6 +332,19 @@
         lax.fori_loop(0, 2, mix_half, 0)
         comb[level + 1][f_me] = hs[level, f_me]
 
+        def drain_dom(k, carry):
+            dom_copy(level, k).wait_send()
+            return carry
+
+        def drain_z(i, carry):
+            z_copy(level, i).wait_send()
+            return carry
+
+        lax.fori_loop(0, n_dom - 1, drain_dom, 0)
+        lax.fori_loop(0, NFEAT - 1, drain_z, 0)
+        if level > 0:
+            lax.fori_loop(0, NFEAT - 1, functools.partial(drain_h, level - 1), 0)
+
         def wait_h(i, carry):
             h_copy(level, 0, i).wait_recv()
             h_copy(level, 1, i).wait_recv()
@@ -331,19 +364,7 @@
     emit_group(LAYERS, f_me, finish)
     lax.fori_loop(0, NFEAT - 1, finish_group, 0)
 
-    for level in range(LAYERS):
-        def drain_dom(k, carry):
-            dom_copy(level, k).wait_send()
-            return carry
-
-        def drain_feat(i, carry):
-            z_copy(level, i).wait_send()
-            h_copy(level, 0, i).wait_send()
-            h_copy(level, 1, i).wait_send()
-            return carry
-
-        lax.fori_loop(0, n_dom - 1, drain_dom, 0)
-        lax.fori_loop(0, NFEAT - 1, drain_feat, 0)
+    lax.fori_loop(0, NFEAT - 1, functools.partial(drain_h, LAYERS - 1), 0)
 
 
 def on_device(
@@ -380,6 +401,7 @@
             pltpu.VMEM((LAYERS, NFEAT, TILE, LANES), BF),
             pltpu.VMEM((LAYERS, NFEAT, TILE, LANES), BF),
             sem((4,)),
+            sem((4,)),
             sem((LAYERS, n_dom - 1)),
             sem((LAYERS, n_dom - 1)),
             sem((LAYERS, NFEAT - 1)),

time: 129 us -> 126 us (0.977)
  Pallas kernels: 127 us -> 124 us
    pallas_call x1, Pallas kernels: 127 us -> 124 us  [on_device(): pl.pallas_call(functools.partial(layer_kernel, n_dom, grid_x, grid_z), ou...]
where the time goes in v4:
time: 126 us
  Pallas kernels  124 us (98%)
  local copies, waits for them, and re-layouts  1.67 us (1%)
    pallas_call x1, Pallas kernels, on_device(): pl.pallas_call(functools.partial(layer_kernel, n_dom, grid_x, grid_z), ou...  124 us

profile of v4, /device:TPU:1, one launch (start us, length us, event | category | flops | bytes accessed | tf_op | source)
XLA Modules:
  0.0 126.0 jit_solution(6569349841347193693)
XLA Ops:
  0.6 123.6 %halo_layers.1 = (bf16[4,32,4096]{2,1,0:T(8,128)(2,1)S(1)}, bf16[32,4096]{1,0:T(8,128)(2,1)S(1)}) custom-call(s32[6,32]{1,0:T(8,128)} %bitcast.15, s32[4,4,8,128]{3,2,1,0:T(8,128)} %bitcast.13, s32[1,32]{1,0:T(1,128)} %counts.1, bf16[128,4096]{1,0:T(8,128)(2,1)} %bitcast.12, bf16[4096,128]{1,0:T(8,128)(2,1)} %feats_hbm.1, bf16[32,128]{1,0:T(8,128)(2,1)} %bitcast.14, ...), custom_call_target="tpu_custom_call" | custom-call | tf_op jit(solution)/shard_map/halo_layers/pallas_call | solution.py:379
  124.3 1.0 copy.12
  125.2 0.7 copy.13

commit v5 on v4

--- a/solution.py
+++ b/solution.py
@@ -101,9 +101,16 @@
 
     barrier = pltpu.get_barrier_semaphore()
 
+    def dest_of(k):
+        i = lax.rem(k, grid_z)
+        half = grid_z // 2
+        dz = jnp.where(lax.rem(i, 2) == 1, half - (i + 1) // 2, half + i // 2)
+        dx = lax.rem(grid_x - 1 - k // grid_z + i + 1, grid_x)
+        return lax.rem(x_me + dx, grid_x) * grid_z + lax.rem(z_me + dz, grid_z)
+
     def greet_dom(i, carry):
         pl.semaphore_signal(
-            barrier, inc=1, device_id=(f_me, lax.rem(d_me + 1 + i, n_dom)), device_id_type=MESH
+            barrier, inc=1, device_id=(f_me, dest_of(i)), device_id_type=MESH
         )
         return carry
 
@@ -137,13 +144,6 @@
     for piece in range(4):
         load_table(piece).wait()
         fill_table(table_t, table, piece)
-
-    def dest_of(k):
-        i = lax.rem(k, grid_z)
-        half = grid_z // 2
-        dz = jnp.where(lax.rem(i, 2) == 1, half - (i + 1) // 2, half + i // 2)
-        dx = lax.rem(grid_x - 1 - k // grid_z + i + 1, grid_x)
-        return lax.rem(x_me + dx, grid_x) * grid_z + lax.rem(z_me + dz, grid_z)
 
     def dom_copy(level, k):
         dest = dest_of(k)
@@ -386,8 +386,8 @@
         out_specs=(vmem, vmem),
         scratch_shapes=[
             pltpu.VMEM((LAYERS * WIDTH, NODES_DEV), BF),
-            pltpu.VMEM((NODES_DEV, LANES), F32),
-            pltpu.VMEM((CAP, LANES), F32),
+            pltpu.VMEM((NODES_DEV + 8, LANES), F32),
+            pltpu.VMEM((CAP + 8, LANES), F32),
             pltpu.VMEM((LAYERS, n_dom, TILE, LANES), BF),
             pltpu.VMEM((PACK, TILE, LANES), BF),
             pltpu.VMEM((LANES, PACK * TILE), BF),

time: 126 us -> 127 us (level)
  no operation moved by 1% of the time
where the time goes in v5:
time: 127 us; the launch traced here: 126 us
  Pallas kernels  124 us (98%)
  local copies, waits for them, and re-layouts  1.67 us (1%)
    pallas_call x1, Pallas kernels, on_device(): pl.pallas_call(functools.partial(layer_kernel, n_dom, grid_x, grid_z), ou...  124 us

profile of v5, /device:TPU:1, one launch (start us, length us, event | category | flops | bytes accessed | tf_op | source)
XLA Modules:
  0.0 126.3 jit_solution(14117894693340032802)
XLA Ops:
  0.6 124.0 %halo_layers.1 = (bf16[4,32,4096]{2,1,0:T(8,128)(2,1)S(1)}, bf16[32,4096]{1,0:T(8,128)(2,1)S(1)}) custom-call(s32[6,32]{1,0:T(8,128)} %bitcast.15, s32[4,4,8,128]{3,2,1,0:T(8,128)} %bitcast.13, s32[1,32]{1,0:T(1,128)} %counts.1, bf16[128,4096]{1,0:T(8,128)(2,1)} %bitcast.12, bf16[4096,128]{1,0:T(8,128)(2,1)} %feats_hbm.1, bf16[32,128]{1,0:T(8,128)(2,1)} %bitcast.14, ...), custom_call_target="tpu_custom_call" | custom-call | tf_op jit(solution)/shard_map/halo_layers/pallas_call | solution.py:379
  124.7 1.0 copy.12
  125.6 0.7 copy.13

commit v6 on v4

--- a/solution.py
+++ b/solution.py
@@ -80,7 +80,7 @@
 def layer_kernel(
     n_dom, grid_x, grid_z,
     columns, rows, counts, table_hbm, feats_hbm, w_in_t, values_hbm, weights_hbm,
-    pushed, final,
+    pushed,
     table_t, table, picked, packed, masks, w_wide,
     comb0, comb1, comb2, comb3, last, initial, feats, values, weights, zs, zr, hs,
     table_sem, load_sem, dom_send, dom_recv, z_send, z_recv, h_send, h_recv,
@@ -354,7 +354,7 @@
             lax.fori_loop(0, NFEAT - 1, wait_h, 0)
 
     def finish(part, start):
-        final[:, pl.ds(start, TILE)] = part
+        pushed[LAYERS, :, pl.ds(start, TILE)] = part
 
     def finish_group(i, carry):
         wait_h(i, 0)
@@ -376,14 +376,13 @@
     smem = pl.BlockSpec(memory_space=pltpu.SMEM)
     hbm = pl.BlockSpec(memory_space=pl.ANY)
     sem = pltpu.SemaphoreType.DMA
-    pushed, final = pl.pallas_call(
+    (rows_t,) = pl.pallas_call(
         functools.partial(layer_kernel, n_dom, grid_x, grid_z),
         out_shape=(
-            pltpu.VMEM((LAYERS, WIDTH, NODES_DEV), BF),
-            pltpu.VMEM((WIDTH, NODES_DEV), BF),
+            pltpu.VMEM((LAYERS + 1, WIDTH, NODES_DEV), BF),
         ),
         in_specs=[smem, smem, smem, hbm, hbm, vmem, hbm, hbm],
-        out_specs=(vmem, vmem),
+        out_specs=(vmem,),
         scratch_shapes=[
             pltpu.VMEM((LAYERS * WIDTH, NODES_DEV), BF),
             pltpu.VMEM((NODES_DEV, LANES), F32),
@@ -415,7 +414,7 @@
         tile_columns.T, send_rows.reshape(n_dom // 8, 8, PACK, TILE).transpose(0, 2, 1, 3), send_counts, table_t, features, w_input.T,
         tile_values, layer_weights,
     )
-    return pushed.transpose(0, 2, 1), final.transpose(1, 0)
+    return rows_t[:LAYERS].transpose(0, 2, 1), rows_t[LAYERS].transpose(1, 0)
 
 
 def solution(mesh):

time: 126 us -> 126 us (level)
    transpose x0 -> x2, local copies, waits for them, and re-layouts: none -> 1.76 us  [on_device(): return (rows_t[:LAYERS].transpose(0, 2, 1), rows_t[LAYERS].transpose(1, 0))]
    unnamed x2 -> x0, local copies, waits for them, and re-layouts: 1.67 us -> none
where the time goes in v6:
time: 126 us
  Pallas kernels  124 us (98%)
  local copies, waits for them, and re-layouts  1.76 us (1%)
    pallas_call x1, Pallas kernels, on_device(): pl.pallas_call(functools.partial(layer_kernel, n_dom, grid_x, grid_z), ou...  124 us

profile of v6, /device:TPU:1, one launch (start us, length us, event | category | flops | bytes accessed | tf_op | source)
XLA Modules:
  0.0 126.0 jit_solution(2786310780545968763)
XLA Ops:
  0.6 123.6 %halo_layers.1 = bf16[5,32,4096]{2,1,0:T(8,128)(2,1)S(1)} custom-call(s32[6,32]{1,0:T(8,128)} %bitcast.17, s32[4,4,8,128]{3,2,1,0:T(8,128)} %bitcast.15, s32[1,32]{1,0:T(1,128)} %counts.1, bf16[128,4096]{1,0:T(8,128)(2,1)} %bitcast.14, bf16[4096,128]{1,0:T(8,128)(2,1)} %feats_hbm.1, bf16[32,128]{1,0:T(8,128)(2,1)} %bitcast.16, ...), custom_call_target="tpu_custom_call" | custom-call | tf_op jit(solution)/shard_map/halo_layers/pallas_call | solution.py:379
  124.3 0.7 slice_bitcast_fusion.1
  125.0 1.0 slice_bitcast_fusion
